TPU v7x, 32 devices: a whole 2x2x4 slice. The times are simulated.
32 devices in a mesh: group: 8 (over y, x, core), shard: 4 (over z).
Axes of the slice: x: 2, y: 2, z: 4, core: 2. Of those that a mesh axis runs over, the one named last changes fastest.
Arguments:
- momentum: bfloat16 [8, 7168, 2048], P(None, ('group', 'shard'))
- gradient: bfloat16 [8, 7168, 2048], P(None, ('group', 'shard'))
- q_prev: bfloat16 [8, 3, 2048, 128], P('group', None, 'shard'), may hold values from -6 to 6
- owner_group: int32 [8], replicated, may hold values from 0 to 7, as said below
- group_counts: int32 [8], replicated, may hold values from 0 to 3, as said below
Outputs:
- momentum_next: bfloat16 [8, 7168, 2048], P(None, ('group', 'shard'))
- update: bfloat16 [8, 7168, 2048], P(None, ('group', 'shard'))
- q_next: bfloat16 [8, 3, 2048, 128], P('group', None, 'shard')
Inputs may be any that keep to these rules, and one draw needn't show every extreme that they name: `owner_group`: each group owns at most 3 experts and some group owns exactly 3; a group's experts fill its slots 0, 1, ... in increasing expert order. `group_counts`: entry g is the number of experts whose owner_group is g, except for one or two groups that own some experts, where it is one less; it equals 3 for some group that owns 3 experts.
All inputs are finite; a program needn't handle non-finite values.
Results may differ from a plain program's by a relative error of at most 0.0059.
Values may be sent and summed in bfloat16 or wider, within the bound.
A program may use at most 128 MiB of HBM per device.

v0:
```python
import math

import jax
import jax.numpy as jnp
from jax import lax
from jax.sharding import PartitionSpec as P

D = 7168
RANK = 128


stability_offset = 1e-06
momentum_decay = 0.6


def owner_slots(owner_group):
    experts = owner_group.shape[0]
    expert_ids = jnp.arange(experts, dtype=jnp.int32)
    same_owner = owner_group[:, None] == owner_group[None, :]
    earlier = expert_ids[None, :] < expert_ids[:, None]
    return jnp.sum((same_owner & earlier).astype(jnp.int32), axis=1)


def pick_table(dest_group, dest_slot, groups, slots):
    targets = jnp.arange(slots * groups, dtype=jnp.int32)
    placed_at = dest_slot * groups + dest_group
    matches = placed_at[None, :] == targets[:, None]
    expert_ids = jnp.arange(dest_group.shape[0], dtype=jnp.int32)
    chosen = jnp.sum(jnp.where(matches, expert_ids[None, :], 0), axis=1)
    occupied_slots = jnp.any(matches, axis=1)
    return (chosen, occupied_slots)


def power_step(blocks, q_full):
    unnormalized_basis = jnp.einsum(
        "srh,shk->srk", blocks, q_full, preferred_element_type=jnp.float32
    )
    left_squares = lax.psum(jnp.sum(unnormalized_basis * unnormalized_basis, axis=1), "shard")
    left_unit = (
        unnormalized_basis * lax.rsqrt(left_squares + stability_offset)[:, None, :]
    ).astype(jnp.bfloat16)
    right_part = jnp.einsum("srh,srk->shk", blocks, left_unit, preferred_element_type=jnp.float32)
    width = right_part.shape[1]
    right_share = lax.psum_scatter(right_part, "shard", scatter_dimension=1, tiled=True)
    right_squares = lax.psum(jnp.sum(right_share * right_share, axis=1), "shard")
    query_factor_share = (
        right_share * lax.rsqrt(right_squares / width + stability_offset)[:, None, :]
    ).astype(jnp.bfloat16)
    right_full, q_new = (
        lax.all_gather(right_share.astype(jnp.bfloat16), "shard", axis=1, tiled=True),
        lax.all_gather(query_factor_share, "shard", axis=1, tiled=True),
    )
    update_multiplier = math.sqrt(D / RANK)
    update_rows = (
        jnp.einsum("srk,shk->srh", left_unit, q_new, preferred_element_type=jnp.float32)
        * update_multiplier
    ).astype(jnp.bfloat16)
    low_rank = jnp.einsum("srk,shk->srh", left_unit, right_full, preferred_element_type=jnp.float32)
    moment_rows = (blocks.astype(jnp.float32) - (1.0 - momentum_decay) * low_rank).astype(
        jnp.bfloat16
    )
    return (moment_rows, update_rows, query_factor_share)


def shards(momentum, gradient, q_prev, owner_group, group_counts):
    groups = lax.axis_size("group")
    current_partition = lax.axis_index("group")
    experts = owner_group.shape[0]
    cap = q_prev.shape[1]
    block = momentum.shape[1]
    hidden = momentum.shape[2]
    share_rows = q_prev.shape[2]
    rank_cols = q_prev.shape[3]
    expert_ids = jnp.arange(experts, dtype=jnp.int32)
    slot_of = owner_slots(owner_group)
    slot_ids = jnp.arange(cap, dtype=jnp.int32)
    live = slot_ids < group_counts[current_partition]
    q_masked = jnp.where(live[:, None, None], q_prev[0], jnp.zeros_like(q_prev[0]))
    combined = (momentum.astype(jnp.float32) + gradient.astype(jnp.float32)).astype(jnp.bfloat16)
    slots = experts // groups
    dest_group = expert_ids % groups
    dest_slot = expert_ids // groups
    chosen, occupied_slots = pick_table(dest_group, dest_slot, groups, slots)
    from_here = occupied_slots & (owner_group[chosen] == current_partition)
    q_send = jnp.where(
        from_here[:, None, None],
        q_masked[slot_of[chosen]],
        jnp.zeros((1, share_rows, rank_cols), jnp.bfloat16),
    )
    q_send = q_send.reshape(slots, groups, share_rows, rank_cols)
    q_recv = lax.all_to_all(q_send, "group", split_axis=1, concat_axis=1, tiled=True)
    stepped = jnp.arange(slots, dtype=jnp.int32) * groups + current_partition
    q_local = q_recv[jnp.arange(slots, dtype=jnp.int32), owner_group[stepped]]
    send_rows = jnp.where(
        occupied_slots[:, None, None], combined[chosen], jnp.zeros((1, block, hidden), jnp.bfloat16)
    )
    send_rows = send_rows.reshape(slots, groups, block, hidden)
    recv_rows = lax.all_to_all(send_rows, "group", split_axis=1, concat_axis=1, tiled=True)
    blocks = recv_rows.reshape(slots, groups * block, hidden)
    q_full = lax.all_gather(q_local, "shard", axis=1, tiled=True)
    moment_rows, update_rows, query_factor_share = power_step(blocks, q_full)
    back_moment, back_update = (
        lax.all_to_all(
            moment_rows.reshape(slots, groups, block, hidden),
            "group",
            split_axis=1,
            concat_axis=1,
            tiled=True,
        ),
        lax.all_to_all(
            update_rows.reshape(slots, groups, block, hidden),
            "group",
            split_axis=1,
            concat_axis=1,
            tiled=True,
        ),
    )
    momentum_next = back_moment[dest_slot, dest_group]
    update = back_update[dest_slot, dest_group]
    owner_chosen, owner_filled = pick_table(owner_group, slot_of, groups, cap)
    from_here = owner_filled & (owner_chosen % groups == current_partition)
    q_send_back = jnp.where(
        from_here[:, None, None],
        query_factor_share[owner_chosen // groups],
        jnp.zeros((1, share_rows, rank_cols), jnp.bfloat16),
    )
    q_send_back = q_send_back.reshape(cap, groups, share_rows, rank_cols)
    q_recv_back = lax.all_to_all(q_send_back, "group", split_axis=1, concat_axis=1, tiled=True)
    local_experts = owner_chosen[slot_ids * groups + current_partition]
    q_owned = q_recv_back[slot_ids, local_experts % groups]
    q_next = jnp.where(live[:, None, None], q_owned, jnp.zeros_like(q_owned))[None]
    return (momentum_next, update, q_next)


def solution(mesh):
    return jax.shard_map(
        shards,
        mesh=mesh,
        in_specs=(
            P(None, ("group", "shard"), None),
            P(None, ("group", "shard"), None),
            P("group", None, "shard", None),
            P(),
            P(),
        ),
        out_specs=(
            P(None, ("group", "shard"), None),
            P(None, ("group", "shard"), None),
            P("group", None, "shard", None),
        ),
        check_vma=False,
    )
```

profile of v0, /device:TPU:0, one launch (start us, length us, event | category | flops | bytes accessed | tf_op | source)
XLA Modules:
  0.0 426.9 jit_solution(14523787279713923337)
XLA Ops:
  7.2 0.1 select_reduce_fusion.1
  7.3 0.1 fusion.5
  7.4 1.2 dynamic_slice.3
  8.7 0.6 iota_compare_fusion.3
  9.3 0.9 convert_reduce_fusion
  10.2 1.3 gather_fusion.1
  11.5 0.6 gather_fusion.2
  12.2 1.1 bitcast_select_fusion.3
  13.3 0.7 gather_fusion.3
  14.1 1.1 bitcast_select_fusion.1
  15.2 5.2 %all-to-all-start.1 = ((bf16[1,8,512,128]{3,2,0,1:T(8,128)(2,1)}), bf16[1,8,512,128]{3,2,0,1:T(8,128)(2,1)S(1)}, u32[]{:S(2)}, u32[]{:S(2)}) async-start(bf16[1,8,512,128]{3,2,0,1:T(8,128)(2,1)} %bitcast_select_fusion.1), calls=%async_computation.1 | async-start | bytes 2097152 | tf_op jit(solution)/shard_map/all_to_all | solution.py:91
  20.4 12.6 %add_convert_fusion = bf16[8,224,2048]{2,1,0:T(8,128)(2,1)} fusion(bf16[8,224,2048]{2,1,0:T(8,128)(2,1)} %param.6, bf16[8,224,2048]{2,1,0:T(8,128)(2,1)} %param.5), kind=kLoop, calls=%fused_computation.10 | loop fusion | flops 14680064 | bytes 22020096 | tf_op jit(solution)/shard_map/convert_element_type | solution.py:79
  33.0 7.1 %gather_fusion = bf16[8,224,2048]{2,1,0:T(8,128)(2,1)} fusion(bf16[8,224,2048]{2,1,0:T(8,128)(2,1)} %add_convert_fusion, s32[1024]{0:T(1024)S(1)} %pad_clamp_fusion.2), kind=kCustom, calls=%fused_computation | custom fusion | bytes 14680096 | tf_op jit(solution)/shard_map/gather | solution.py:95
  40.2 6.7 %bitcast_select_fusion = bf16[1,8,224,2048]{3,2,0,1:T(8,128)(2,1)} fusion(bf16[8,224,2048]{2,1,0:T(8,128)(2,1)} %gather_fusion, pred[8]{0:T(512)(128)(4,1)S(1)} %fusion.5), kind=kLoop, calls=%fused_computation.11 | loop fusion | flops 3670016 | bytes 14680072 | tf_op jit(solution)/shard_map/jit(_where)/select_n | solution.py:94
  46.9 0.0 copy-start
  46.9 0.0 all-to-all-done.1
  46.9 5.0 %all-to-all-start = ((bf16[1,8,224,2048]{3,2,0,1:T(8,128)(2,1)}), bf16[1,8,224,2048]{3,2,0,1:T(8,128)(2,1)}, u32[]{:S(2)}, u32[]{:S(2)}) async-start(bf16[1,8,224,2048]{3,2,0,1:T(8,128)(2,1)} %bitcast_select_fusion), calls=%async_computation | async-start | bytes 14680064 | tf_op jit(solution)/shard_map/all_to_all | solution.py:98
  51.9 0.0 reduce-scatter.2.cloned.1.call-start
  51.9 0.0 copy-done
  51.9 0.7 dynamic-slice.5
  54.7 16.5 %all-gather = bf16[1,1,2048,128]{3,2,0,1:T(8,128)(2,1)S(1)} all-gather(bf16[1,1,512,128]{3,2,0,1:T(8,128)(2,1)S(1)} %constant_dynamic-slice_fusion), channel_id=2, replica_groups=mesh['group'=8,'shard'=4] {'shard'}, dimensions={2}, use_global_device_ids=true | all-gather | bytes 655360 | tf_op jit(solution)/shard_map/all_gather | solution.py:100
  71.1 63.5 %all-to-all-done = bf16[1,8,224,2048]{3,2,0,1:T(8,128)(2,1)} async-done(((bf16[1,8,224,2048]{3,2,0,1:T(8,128)(2,1)}), bf16[1,8,224,2048]{3,2,0,1:T(8,128)(2,1)}, u32[]{:S(2)}, u32[]{:S(2)}) %all-to-all-start) | async-done | bytes 7340064 | tf_op jit(solution)/shard_map/all_to_all | solution.py:98
  134.7 5.2 %multiply_reduce_fusion = (f32[128]{0:T(128)S(1)}, f32[1792,128]{1,0:T(8,128)S(1)}) fusion(bf16[1792,2048]{1,0:T(8,128)(2,1)} %bitcast.3, bf16[1,1,2048,128]{3,2,0,1:T(8,128)(2,1)S(1)} %all-gather), kind=kOutput, calls=%fused_computation.16 | convolution fusion | flops 939982720 | bytes 8782336 | tf_op jit(solution)/shard_map/srh,shk->srk/dot_general | solution.py:35
  139.9 12.0 %psum.14 = f32[1,128]{1,0:T(1,128)S(1)} all-reduce(f32[1,128]{1,0:T(1,128)S(1)} %bitcast.68), channel_id=1, replica_groups=mesh['group'=8,'shard'=4] {'shard'}, use_global_device_ids=true, to_apply=%region_4.5 | all-reduce | flops 128 | bytes 1024 | tf_op jit(solution)/shard_map/psum | solution.py:38
  151.8 0.1 multiply_convert_fusion.1
  151.9 6.2 %convolution_bitcast_fusion = f32[1,2048,128]{2,1,0:T(8,128)} fusion(bf16[1792,2048]{1,0:T(8,128)(2,1)} %bitcast.3, bf16[1792,128]{1,0:T(8,128)(2,1)S(1)} %multiply_convert_fusion.1), kind=kOutput, calls=%fused_computation.13 | convolution fusion | flops 939524096 | bytes 8847360 | tf_op jit(solution)/shard_map/srh,srk->shk/dot_general | solution.py:42
  158.1 0.0 reduce-scatter.2.cloned.1.call-update
  158.1 0.1 fusion.4
  158.2 0.1 reduce_or.22
  158.3 0.1 select_reduce_fusion
  158.4 0.1 reduce_sum.63
  158.5 0.1 copy.17
  158.6 23.4 %reduce-scatter.2.cloned.1.call-done = f32[1,512,128]{2,1,0:T(8,128)} async-done(((f32[1,2048,128]{2,1,0:T(8,128)}), f32[1,512,128]{2,1,0:T(8,128)}) %reduce-scatter.2.cloned.1.call-update) | async-done | bytes 262160 | tf_op jit(solution)/shard_map/reduce_scatter | solution.py:44
  182.0 1.0 multiply_reduce_fusion.1
  183.0 9.3 %psum.15 = f32[1,128]{1,0:T(1,128)S(1)} all-reduce(f32[1,128]{1,0:T(1,128)S(1)} %bitcast.67), channel_id=1, replica_groups=mesh['group'=8,'shard'=4] {'shard'}, use_global_device_ids=true, to_apply=%region_7.8 | all-reduce | flops 128 | bytes 1024 | tf_op jit(solution)/shard_map/psum | solution.py:45
  192.3 1.1 multiply_convert_fusion.2
  193.3 1.9 broadcast_select_fusion
  195.3 4.4 %all-to-all-start.4 = ((bf16[3,8,512,128]{3,2,0,1:T(8,128)(2,1)}), bf16[3,8,512,128]{3,2,0,1:T(8,128)(2,1)}, u32[]{:S(2)}, u32[]{:S(2)}) async-start(bf16[3,8,512,128]{3,2,0,1:T(8,128)(2,1)} %broadcast_select_fusion), calls=%async_computation.5 | async-start | bytes 6291456 | tf_op jit(solution)/shard_map/all_to_all | solution.py:128
  199.7 16.4 %all_gather.10 = bf16[1,2048,128]{2,1,0:T(8,128)(2,1)S(1)} all-gather(bf16[1,512,128]{2,1,0:T(8,128)(2,1)S(1)} %get-tuple-element.26), channel_id=1, replica_groups=mesh['group'=8,'shard'=4] {'shard'}, dimensions={1}, use_global_device_ids=true | all-gather | bytes 655360 | tf_op jit(solution)/shard_map/all_gather | solution.py:50
  216.1 8.3 %subtract_convert_fusion = bf16[1792,2048]{1,0:T(8,128)(2,1)} fusion(bf16[1792,2048]{1,0:T(8,128)(2,1)} %bitcast.3, bf16[1792,128]{1,0:T(8,128)(2,1)S(1)} %multiply_convert_fusion.1, bf16[1,2048,128]{2,1,0:T(8,128)(2,1)S(1)} %all_gather.10), kind=kOutput, calls=%fused_computation.9 | convolution fusion | flops 954204160 | bytes 15663104 | tf_op jit(solution)/shard_map/srk,shk->srh/dot_general | solution.py:58
  224.4 13.2 %all-to-all-done.4 = bf16[3,8,512,128]{3,2,0,1:T(8,128)(2,1)} async-done(((bf16[3,8,512,128]{3,2,0,1:T(8,128)(2,1)}), bf16[3,8,512,128]{3,2,0,1:T(8,128)(2,1)}, u32[]{:S(2)}, u32[]{:S(2)}) %all-to-all-start.4) | async-done | bytes 3145760 | tf_op jit(solution)/shard_map/all_to_all | solution.py:128
  237.6 4.8 %all-to-all-start.2 = ((bf16[1,8,224,2048]{3,2,0,1:T(8,128)(2,1)}), bf16[1,8,224,2048]{3,2,0,1:T(8,128)(2,1)}, u32[]{:S(2)}, u32[]{:S(2)}) async-start(bf16[1,8,224,2048]{3,2,0,1:T(8,128)(2,1)} %bitcast.64), calls=%async_computation.3 | async-start | bytes 14680064 | tf_op jit(solution)/shard_map/all_to_all | solution.py:103
  242.4 16.2 %all_gather.11 = bf16[1,2048,128]{2,1,0:T(8,128)(2,1)S(1)} all-gather(bf16[1,512,128]{2,1,0:T(8,128)(2,1)S(1)} %get-tuple-element.25), channel_id=1, replica_groups=mesh['group'=8,'shard'=4] {'shard'}, dimensions={1}, use_global_device_ids=true | all-gather | bytes 655360 | tf_op jit(solution)/shard_map/all_gather | solution.py:51
  258.7 5.0 %multiply_convert_fusion = bf16[1792,2048]{1,0:T(8,128)(2,1)} fusion(bf16[1792,128]{1,0:T(8,128)(2,1)S(1)} %multiply_convert_fusion.1, bf16[1,2048,128]{2,1,0:T(8,128)(2,1)S(1)} %all_gather.11), kind=kOutput, calls=%fused_computation.8 | convolution fusion | flops 946864128 | bytes 8323072 | tf_op jit(solution)/shard_map/srk,shk->srh/dot_general | solution.py:55
  263.7 61.6 %all-to-all-done.2 = bf16[1,8,224,2048]{3,2,0,1:T(8,128)(2,1)} async-done(((bf16[1,8,224,2048]{3,2,0,1:T(8,128)(2,1)}), bf16[1,8,224,2048]{3,2,0,1:T(8,128)(2,1)}, u32[]{:S(2)}, u32[]{:S(2)}) %all-to-all-start.2) | async-done | bytes 7340064 | tf_op jit(solution)/shard_map/all_to_all | solution.py:103
  325.3 4.8 %all-to-all-start.3 = ((bf16[1,8,224,2048]{3,2,0,1:T(8,128)(2,1)}), bf16[1,8,224,2048]{3,2,0,1:T(8,128)(2,1)}, u32[]{:S(2)}, u32[]{:S(2)}) async-start(bf16[1,8,224,2048]{3,2,0,1:T(8,128)(2,1)} %bitcast.65), calls=%async_computation.4 | async-start | bytes 14680064 | tf_op jit(solution)/shard_map/all_to_all | solution.py:110
  330.1 0.6 gather_fusion.6
  330.8 2.5 gather_fusion.7
  333.3 0.8 bitcast_select_fusion.2
  334.2 7.1 %gather_fusion.4 = bf16[8,224,2048]{2,1,0:T(8,128)(2,1)} fusion(bf16[1,8,224,2048]{3,2,1,0:T(8,128)(2,1)} %bitcast.19, s32[8]{0:T(128)S(1)} %fusion.14), kind=kCustom, calls=%fused_computation.4 | custom fusion | bytes 14680128 | tf_op jit(solution)/shard_map/gather | solution.py:118
  341.3 71.6 %all-to-all-done.3 = bf16[1,8,224,2048]{3,2,0,1:T(8,128)(2,1)} async-done(((bf16[1,8,224,2048]{3,2,0,1:T(8,128)(2,1)}), bf16[1,8,224,2048]{3,2,0,1:T(8,128)(2,1)}, u32[]{:S(2)}, u32[]{:S(2)}) %all-to-all-start.3) | async-done | bytes 7340064 | tf_op jit(solution)/shard_map/all_to_all | solution.py:110
  412.9 7.1 %gather_fusion.5 = bf16[8,224,2048]{2,1,0:T(8,128)(2,1)} fusion(bf16[1,8,224,2048]{3,2,1,0:T(8,128)(2,1)} %bitcast.26, s32[8]{0:T(128)S(1)} %fusion.14), kind=kCustom, calls=%fused_computation.5 | custom fusion | bytes 14680128 | tf_op jit(solution)/shard_map/gather | solution.py:119
  (15 shorter events, 0.1 us)
Async XLA Ops:
  15.2 31.7 %all-to-all-start.1 = ((bf16[1,8,512,128]{3,2,0,1:T(8,128)(2,1)}), bf16[1,8,512,128]{3,2,0,1:T(8,128)(2,1)S(1)}, u32[]{:S(2)}, u32[]{:S(2)}) async-start(bf16[1,8,512,128]{3,2,0,1:T(8,128)(2,1)} %bitcast_select_fusion.1), calls=%async_computation.1 | async-start | bytes 2097152 | tf_op jit(solution)/shard_map/all_to_all | solution.py:91
  46.9 5.0 %copy-start = (s32[8]{0:T(128)S(1)}, s32[8]{0:T(128)}, u32[]{:S(2)}) copy-start(s32[8]{0:T(128)} %param.8) | copy-start | bytes 100
  46.9 87.8 %all-to-all-start = ((bf16[1,8,224,2048]{3,2,0,1:T(8,128)(2,1)}), bf16[1,8,224,2048]{3,2,0,1:T(8,128)(2,1)}, u32[]{:S(2)}, u32[]{:S(2)}) async-start(bf16[1,8,224,2048]{3,2,0,1:T(8,128)(2,1)} %bitcast_select_fusion), calls=%async_computation | async-start | bytes 14680064 | tf_op jit(solution)/shard_map/all_to_all | solution.py:98
  51.9 130.1 %reduce-scatter.2.cloned.1.call-start = ((), (), s32[]{:S(2)}) async-start(), calls=%async_computation.6 | async-start | bytes 1310720 | tf_op jit(solution)/shard_map/reduce_scatter | solution.py:44
  195.3 42.3 %all-to-all-start.4 = ((bf16[3,8,512,128]{3,2,0,1:T(8,128)(2,1)}), bf16[3,8,512,128]{3,2,0,1:T(8,128)(2,1)}, u32[]{:S(2)}, u32[]{:S(2)}) async-start(bf16[3,8,512,128]{3,2,0,1:T(8,128)(2,1)} %broadcast_select_fusion), calls=%async_computation.5 | async-start | bytes 6291456 | tf_op jit(solution)/shard_map/all_to_all | solution.py:128
  237.6 87.7 %all-to-all-start.2 = ((bf16[1,8,224,2048]{3,2,0,1:T(8,128)(2,1)}), bf16[1,8,224,2048]{3,2,0,1:T(8,128)(2,1)}, u32[]{:S(2)}, u32[]{:S(2)}) async-start(bf16[1,8,224,2048]{3,2,0,1:T(8,128)(2,1)} %bitcast.64), calls=%async_computation.3 | async-start | bytes 14680064 | tf_op jit(solution)/shard_map/all_to_all | solution.py:103
  325.3 87.6 %all-to-all-start.3 = ((bf16[1,8,224,2048]{3,2,0,1:T(8,128)(2,1)}), bf16[1,8,224,2048]{3,2,0,1:T(8,128)(2,1)}, u32[]{:S(2)}, u32[]{:S(2)}) async-start(bf16[1,8,224,2048]{3,2,0,1:T(8,128)(2,1)} %bitcast.65), calls=%async_computation.4 | async-start | bytes 14680064 | tf_op jit(solution)/shard_map/all_to_all | solution.py:110
Sparse Core Ops, SparseCore 0:
  158.2 23.6 reduce-scatter.1
where the time goes:
time: 428 us; the launch traced here: 427 us
  waiting for transfers between devices  233 us (54%)
  blocking collectives  70.3 us (16%)
  local copies, waits for them, and re-layouts  29.5 us (7%)
  other arithmetic  28.5 us (7%)
  matrix products  24.7 us (6%)
  starting transfers between devices  24.3 us (6%)
  between operations  16.3 us (4%)
    all_to_all x1, waiting for transfers between devices, shards(): lax.all_to_all(update_rows.reshape(slots, groups, block, hidden), 'group'...  71.6 us
    all_to_all x1, waiting for transfers between devices, shards(): lax.all_to_all(send_rows, 'group', split_axis=1, concat_axis=1, tiled=True)  63.5 us
    all_to_all x1, waiting for transfers between devices, shards(): lax.all_to_all(moment_rows.reshape(slots, groups, block, hidden), 'group'...  61.6 us
    reduce_scatter x1, waiting for transfers between devices, power_step(): lax.psum_scatter(right_part, 'shard', scatter_dimension=1, tiled=True)  23.4 us
    all_gather x1, blocking collectives, shards(): q_full = lax.all_gather(q_local, 'shard', axis=1, tiled=True)  16.5 us
    all_gather x1, blocking collectives, power_step(): lax.all_gather(right_share.astype(jnp.bfloat16), 'shard', axis=1, tiled=T...  16.4 us
    all_gather x1, blocking collectives, power_step(): lax.all_gather(query_factor_share, 'shard', axis=1, tiled=True)  16.2 us
    all_to_all x1, waiting for transfers between devices, shards(): lax.all_to_all(q_send_back, 'group', split_axis=1, concat_axis=1, tiled=T...  13.2 us
  transfers between devices with their start and end apart: 6, of which 5 were waited for; matrix products, arithmetic and copies ran while one was open for 12% of the time, Pallas kernels for 0%

commit v1 on v0

v1 whole, which is shorter than its diff:
```python
import math

import jax
import jax.numpy as jnp
from jax import lax
from jax.sharding import PartitionSpec as P

D = 7168
RANK = 128

stability_offset = 1e-06
momentum_decay = 0.6
AXES = ("group", "shard")


def owner_slots(owner_group):
    experts = owner_group.shape[0]
    expert_ids = jnp.arange(experts, dtype=jnp.int32)
    same_owner = owner_group[:, None] == owner_group[None, :]
    earlier = expert_ids[None, :] < expert_ids[:, None]
    return jnp.sum((same_owner & earlier).astype(jnp.int32), axis=1)


def shards(momentum, gradient, q_prev, owner_group, group_counts):
    me = lax.axis_index("group")
    experts, block, hidden = momentum.shape
    cap, share_rows, rank = q_prev.shape[1:]
    slot_of = owner_slots(owner_group)
    keep = slot_of < group_counts[owner_group]
    mine = keep & (owner_group == me)

    pieces = jnp.zeros((experts, share_rows, rank), jnp.bfloat16)
    for j in range(cap):
        pick = mine & (slot_of == j)
        pieces = jnp.where(pick[:, None, None], q_prev[0, j][None], pieces)
    q_one = lax.psum_scatter(pieces, "group", scatter_dimension=0, tiled=True)
    q_shard = lax.all_gather(q_one, "shard", axis=1, tiled=True)
    q_full = lax.all_gather(q_shard, "group", axis=0, tiled=True)

    combined = (momentum.astype(jnp.float32) + gradient.astype(jnp.float32)).astype(jnp.bfloat16)
    left_raw = jnp.einsum("erh,ehk->erk", combined, q_full, preferred_element_type=jnp.float32)
    squares = lax.psum(jnp.sum(left_raw * left_raw, axis=1), AXES)
    left_unit = (left_raw * lax.rsqrt(squares + stability_offset)[:, None, :]).astype(jnp.bfloat16)
    part = jnp.einsum("erh,erk->ehk", combined, left_unit, preferred_element_type=jnp.float32)

    part = lax.psum_scatter(part, "group", scatter_dimension=0, tiled=True)
    share = lax.psum_scatter(part, "shard", scatter_dimension=1, tiled=True)
    right = lax.all_gather(share.astype(jnp.bfloat16), "shard", axis=1, tiled=True)
    right = lax.all_gather(right, "group", axis=0, tiled=True)

    right32 = right.astype(jnp.float32)
    scale = lax.rsqrt(jnp.mean(right32 * right32, axis=1) + stability_offset)
    q_new = (right32 * scale[:, None, :]).astype(jnp.bfloat16)
    update = (
        jnp.einsum("erk,ehk->erh", left_unit, q_new, preferred_element_type=jnp.float32)
        * math.sqrt(D / RANK)
    ).astype(jnp.bfloat16)
    low_rank = jnp.einsum("erk,ehk->erh", left_unit, right, preferred_element_type=jnp.float32)
    momentum_next = (
        combined.astype(jnp.float32) - (1.0 - momentum_decay) * low_rank
    ).astype(jnp.bfloat16)

    rows = lax.dynamic_slice_in_dim(q_new, lax.axis_index("shard") * share_rows, share_rows, axis=1)
    kept = []
    for j in range(cap):
        pick = mine & (slot_of == j)
        kept.append(jnp.sum(jnp.where(pick[:, None, None], rows, jnp.zeros_like(rows)), axis=0))
    return (momentum_next, update, jnp.stack(kept)[None])


def solution(mesh):
    return jax.shard_map(
        shards,
        mesh=mesh,
        in_specs=(
            P(None, AXES, None),
            P(None, AXES, None),
            P("group", None, "shard", None),
            P(),
            P(),
        ),
        out_specs=(P(None, AXES, None), P(None, AXES, None), P("group", None, "shard", None)),
        check_vma=False,
    )
```

time: 428 us -> 347 us (0.81)
  local copies, waits for them, and re-layouts: 29.5 us -> 1.72 us
  starting transfers between devices: 24.3 us -> 0.2 us
  waiting for transfers between devices: 233 us -> 211 us
  other arithmetic: 28.5 us -> 12.1 us
  matrix products: 24.7 us -> 34.2 us
    all_to_all x5 -> x0, waiting for transfers between devices: 210 us -> none  [the longest x1 71.6 us: shards(): lax.all_to_all(update_rows.reshape(slots, groups, block, hidden), 'group'...]
    reduce_scatter x1 -> x3, waiting for transfers between devices: 23.4 us -> 141 us  [the longest x1 72.4 us: shards(): part = lax.psum_scatter(part, 'group', scatter_dimension=0, tiled=True)]
    all_gather x0 -> x2, waiting for transfers between devices: none -> 70.8 us  [the longest x1 35.9 us: shards(): q_full = lax.all_gather(q_shard, 'group', axis=0, tiled=True)]
    gather x9 -> x1, local copies, waits for them, and re-layouts: 28 us -> 0.64 us  [shards(): keep = slot_of < group_counts[owner_group]]
    all_to_all x5 -> x0, starting transfers between devices: 24.3 us -> none  [the longest x1 5.2 us: shards(): lax.all_to_all(q_send, 'group', split_axis=1, concat_axis=1, tiled=True)]
    psum x2 -> x1, blocking collectives: 21.2 us -> 39.3 us  [shards(): squares = lax.psum(jnp.sum(left_raw * left_raw, axis=1), AXES)]
    all_gather x3 -> x2, blocking collectives: 49.1 us -> 34 us  [the longest x1 17.1 us: shards(): q_shard = lax.all_gather(q_one, 'shard', axis=1, tiled=True)]
    select_n x8 -> x2, other arithmetic: 11.7 us -> 1.85 us  [the longest x1 1.2 us: shards(): pieces = jnp.where(pick[:, None, None], q_prev[0, j][None], pieces)]
  transfers between devices with their start and end apart: 6 -> 5, of which waited for: 5 -> 5; matrix products, arithmetic and copies ran while one was open for 12% -> 0% of each run, Pallas kernels for 0% -> 0%
where the time goes in v1:
time: 347 us
  waiting for transfers between devices  211 us (61%)
  blocking collectives  73.3 us (21%)
  matrix products  34.2 us (10%)
  between operations  13.8 us (4%)
  other arithmetic  12.1 us (3%)
    reduce_scatter x1, waiting for transfers between devices, shards(): part = lax.psum_scatter(part, 'group', scatter_dimension=0, tiled=True)  72.4 us
    psum x1, blocking collectives, shards(): squares = lax.psum(jnp.sum(left_raw * left_raw, axis=1), AXES)  39.3 us
    reduce_scatter x1, waiting for transfers between devices, shards(): q_one = lax.psum_scatter(pieces, 'group', scatter_dimension=0, tiled=True)  38.8 us
    all_gather x1, waiting for transfers between devices, shards(): q_full = lax.all_gather(q_shard, 'group', axis=0, tiled=True)  35.9 us
    all_gather x1, waiting for transfers between devices, shards(): right = lax.all_gather(right, 'group', axis=0, tiled=True)  34.9 us
    reduce_scatter x1, waiting for transfers between devices, shards(): share = lax.psum_scatter(part, 'shard', scatter_dimension=1, tiled=True)  29.4 us
    all_gather x1, blocking collectives, shards(): q_shard = lax.all_gather(q_one, 'shard', axis=1, tiled=True)  17.1 us
    all_gather x1, blocking collectives, shards(): lax.all_gather(share.astype(jnp.bfloat16), 'shard', axis=1, tiled=True)  16.8 us
  transfers between devices with their start and end apart: 5, of which 5 were waited for; matrix products, arithmetic and copies ran while one was open for 0% of the time, Pallas kernels for 0%

profile of v1, /device:TPU:0, one launch (start us, length us, event | category | flops | bytes accessed | tf_op | source)
XLA Modules:
  0.0 346.7 jit_solution(16092060516255264329)
XLA Ops:
  7.2 0.0 copy-start
  7.2 0.0 reduce-scatter.4.cloned.1.call-start
  7.2 0.9 convert_reduce_fusion
  8.1 0.7 compare_select_fusion
  8.8 0.0 copy-done
  8.8 0.6 gather_fusion
  9.5 0.7 compare_and_fusion.2
  10.1 1.1 slice_bitcast_fusion.2
  11.2 1.2 select_select_fusion
  12.4 0.0 reduce-scatter.4.cloned.1.call-update
  12.4 0.0 all-gather.3.cloned.1.call-start
  12.5 38.8 %reduce-scatter.4.cloned.1.call-done = bf16[1,512,128]{2,1,0:T(8,128)(2,1)} async-done(((bf16[8,512,128]{2,1,0:T(8,128)(2,1)}), bf16[1,512,128]{2,1,0:T(8,128)(2,1)}) %reduce-scatter.4.cloned.1.call-update) | async-done | bytes 131088 | tf_op jit(solution)/shard_map/reduce_scatter | solution.py:36
  51.3 17.1 %all_gather.12 = bf16[1,2048,128]{2,1,0:T(8,128)(2,1)} all-gather(bf16[1,512,128]{2,1,0:T(8,128)(2,1)} %reduce-scatter.4.cloned.1.call-done), channel_id=1, replica_groups=mesh['group'=8,'shard'=4] {'shard'}, dimensions={1}, use_global_device_ids=true | all-gather | bytes 655360 | tf_op jit(solution)/shard_map/all_gather | solution.py:37
  68.4 0.0 all-gather.3.cloned.1.call-update
  68.4 0.0 reduce-scatter.6.cloned.1.call-start
  68.5 35.9 %all-gather.3.cloned.1.call-done = bf16[8,2048,128]{2,1,0:T(8,128)(2,1)} async-done(((bf16[1,2048,128]{2,1,0:T(8,128)(2,1)}), bf16[8,2048,128]{2,1,0:T(8,128)(2,1)}) %all-gather.3.cloned.1.call-update) | async-done | bytes 4194320 | tf_op jit(solution)/shard_map/all_gather | solution.py:38
  104.4 8.7 %multiply_reduce_fusion = (f32[8,128]{1,0:T(8,128)S(1)}, f32[8,224,128]{2,1,0:T(8,128)S(1)}) fusion(bf16[8,2048,128]{2,1,0:T(8,128)(2,1)} %all-gather.3.cloned.1.call-done, bf16[8,224,2048]{2,1,0:T(8,128)(2,1)} %param.6, bf16[8,224,2048]{2,1,0:T(8,128)(2,1)} %param.5), kind=kOutput, calls=%fused_computation.13 | convolution fusion | flops 954661888 | bytes 19795968 | tf_op jit(solution)/shard_map/erh,ehk->erk/dot_general | solution.py:41
  113.1 39.3 %psum.7 = f32[8,128]{1,0:T(8,128)S(1)} all-reduce(f32[8,128]{1,0:T(8,128)S(1)} %get-tuple-element.13), channel_id=1, replica_groups=mesh['group'=8,'shard'=4] {'group','shard'}, use_global_device_ids=true, to_apply=%region_3.4 | all-reduce | flops 1024 | bytes 8192 | tf_op jit(solution)/shard_map/psum | solution.py:42
  152.4 0.1 multiply_convert_fusion.1
  152.5 11.6 %fusion.3 = f32[8,2048,128]{2,1,0:T(8,128)} fusion(bf16[8,224,128]{2,1,0:T(8,128)(2,1)S(1)} %multiply_convert_fusion.1, bf16[8,224,2048]{2,1,0:T(8,128)(2,1)} %param.6, bf16[8,224,2048]{2,1,0:T(8,128)(2,1)} %param.5), kind=kOutput, calls=%fused_computation.29 | convolution fusion | flops 954204160 | bytes 23527424 | tf_op jit(solution)/shard_map/erh,erk->ehk/dot_general | solution.py:44
  164.1 0.0 reduce-scatter.6.cloned.1.call-update
  164.1 0.0 reduce-scatter.8.cloned.1.call-start
  164.2 72.4 %reduce-scatter.6.cloned.1.call-done = f32[1,2048,128]{2,1,0:T(8,128)} async-done(((f32[8,2048,128]{2,1,0:T(8,128)}), f32[1,2048,128]{2,1,0:T(8,128)}) %reduce-scatter.6.cloned.1.call-update) | async-done | bytes 1048592 | tf_op jit(solution)/shard_map/reduce_scatter | solution.py:46
  236.6 0.0 reduce-scatter.8.cloned.1.call-update
  236.6 0.0 all-gather.5.cloned.1.call-start
  236.6 29.4 %reduce-scatter.8.cloned.1.call-done = f32[1,512,128]{2,1,0:T(8,128)} async-done(((f32[1,2048,128]{2,1,0:T(8,128)}), f32[1,512,128]{2,1,0:T(8,128)}) %reduce-scatter.8.cloned.1.call-update) | async-done | bytes 262160 | tf_op jit(solution)/shard_map/reduce_scatter | solution.py:47
  266.0 1.0 convert_element_type.45
  267.0 16.8 %all_gather.14 = bf16[1,2048,128]{2,1,0:T(8,128)(2,1)} all-gather(bf16[1,512,128]{2,1,0:T(8,128)(2,1)S(1)} %convert_element_type.45), channel_id=1, replica_groups=mesh['group'=8,'shard'=4] {'shard'}, dimensions={1}, use_global_device_ids=true | all-gather | bytes 655360 | tf_op jit(solution)/shard_map/all_gather | solution.py:48
  283.8 0.0 all-gather.5.cloned.1.call-update
  283.8 34.9 %all-gather.5.cloned.1.call-done = bf16[8,2048,128]{2,1,0:T(8,128)(2,1)} async-done(((bf16[1,2048,128]{2,1,0:T(8,128)(2,1)}), bf16[8,2048,128]{2,1,0:T(8,128)(2,1)}) %all-gather.5.cloned.1.call-update) | async-done | bytes 4194320 | tf_op jit(solution)/shard_map/all_gather | solution.py:49
  318.8 3.0 fusion
  321.8 3.1 fusion.1
  324.9 0.0 copy-start.1
  324.9 5.1 %multiply_convert_fusion = bf16[8,224,2048]{2,1,0:T(8,128)(2,1)} fusion(bf16[8,224,128]{2,1,0:T(8,128)(2,1)S(1)} %multiply_convert_fusion.1, bf16[8,2048,128]{2,1,0:T(8,128)(2,1)S(1)} %fusion.1), kind=kOutput, calls=%fused_computation.1 | convolution fusion | flops 946864128 | bytes 11993088 | tf_op jit(solution)/shard_map/erk,ehk->erh/dot_general | solution.py:55
  330.1 0.6 select_reduce_fusion.2
  330.7 0.8 maximum_bitcast_fusion
  331.5 0.0 copy-done.1
  331.5 8.7 %subtract_convert_fusion = bf16[8,224,2048]{2,1,0:T(8,128)(2,1)} fusion(bf16[8,224,128]{2,1,0:T(8,128)(2,1)S(1)} %multiply_convert_fusion.1, bf16[8,2048,128]{2,1,0:T(8,128)(2,1)S(1)} %copy-done.1, bf16[8,224,2048]{2,1,0:T(8,128)(2,1)} %param.6, bf16[8,224,2048]{2,1,0:T(8,128)(2,1)} %param.5), kind=kOutput, calls=%fused_computation.2 | convolution fusion | flops 968884224 | bytes 26673152 | tf_op jit(solution)/shard_map/erk,ehk->erh/dot_general | solution.py:58
  (4 shorter events, 0.0 us)
Async XLA Ops:
  7.2 1.6 copy-start
  7.2 44.1 %reduce-scatter.4.cloned.1.call-start = ((), (), s32[]{:S(2)}) async-start(), calls=%async_computation.3 | async-start | bytes 1179648 | tf_op jit(solution)/shard_map/reduce_scatter | solution.py:36
  12.4 91.9 %all-gather.3.cloned.1.call-start = ((), (), s32[]{:S(2)}) async-start(), calls=%async_computation.4 | async-start | bytes 4718592 | tf_op jit(solution)/shard_map/all_gather | solution.py:38
  68.4 168.1 %reduce-scatter.6.cloned.1.call-start = ((), (), s32[]{:S(2)}) async-start(), calls=%async_computation.5 | async-start | bytes 9437184 | tf_op jit(solution)/shard_map/reduce_scatter | solution.py:46
  164.1 101.9 %reduce-scatter.8.cloned.1.call-start = ((), (), s32[]{:S(2)}) async-start(), calls=%async_computation.6 | async-start | bytes 1310720 | tf_op jit(solution)/shard_map/reduce_scatter | solution.py:47
  236.6 82.2 %all-gather.5.cloned.1.call-start = ((), (), s32[]{:S(2)}) async-start(), calls=%async_computation.7 | async-start | bytes 4718592 | tf_op jit(solution)/shard_map/all_gather | solution.py:49
  324.9 6.6 %copy-start.1 = (bf16[8,2048,128]{2,1,0:T(8,128)(2,1)S(1)}, bf16[8,2048,128]{2,1,0:T(8,128)(2,1)}, u32[]{:S(2)}) copy-start(bf16[8,2048,128]{2,1,0:T(8,128)(2,1)} %all-gather.5.cloned.1.call-done) | copy-start | bytes 12582916
Sparse Core Ops, SparseCore 0:
  12.5 38.6 reduce-scatter.3
  68.5 35.7 all-gather.2
  164.3 72.2 reduce-scatter.5
  238.7 27.2 reduce-scatter.7
  283.9 34.7 all-gather.4

commit v2 on v1

--- a/solution.py
+++ b/solution.py
@@ -3,6 +3,8 @@
 import jax
 import jax.numpy as jnp
 from jax import lax
+from jax.experimental import pallas as pl
+from jax.experimental.pallas import tpu as pltpu
 from jax.sharding import PartitionSpec as P
 
 D = 7168
@@ -21,6 +23,99 @@
     return jnp.sum((same_owner & earlier).astype(jnp.int32), axis=1)
 
 
+def exchange_sum(x, place, n, split, collective_id):
+    rows, cols = x.shape[-2:]
+    step = min(rows, 128)
+
+    def kernel(x_ref, o_ref, landed, send_sem, recv_sem):
+        me, peer = place()
+
+        def copy(k):
+            at = lax.rem(me + k, n)
+            return pltpu.make_async_remote_copy(
+                src_ref=x_ref.at[at] if split else x_ref,
+                dst_ref=landed.at[k - 1],
+                send_sem=send_sem.at[k - 1],
+                recv_sem=recv_sem.at[k - 1],
+                device_id=peer(at),
+                device_id_type=pl.DeviceIdType.MESH,
+            )
+
+        barrier = pltpu.get_barrier_semaphore()
+
+        @pl.loop(1, n)
+        def _(k):
+            pl.semaphore_signal(
+                barrier,
+                inc=1,
+                device_id=peer(lax.rem(me + k, n)),
+                device_id_type=pl.DeviceIdType.MESH,
+            )
+
+        pl.semaphore_wait(barrier, n - 1)
+
+        @pl.loop(1, n)
+        def _(k):
+            copy(k).start()
+
+        @pl.loop(1, n)
+        def _(k):
+            copy(k).wait()
+
+        @pl.loop(0, rows // step)
+        def _(i):
+            span = pl.ds(pl.multiple_of(i * step, step), step)
+            own = x_ref[me, span, :] if split else x_ref[span, :]
+            total = own.astype(jnp.float32)
+            for k in range(n - 1):
+                total = total + landed[k, span, :].astype(jnp.float32)
+            o_ref[span, :] = total.astype(o_ref.dtype)
+
+    return pl.pallas_call(
+        kernel,
+        out_shape=jax.ShapeDtypeStruct((rows, cols), x.dtype),
+        in_specs=[pl.BlockSpec(memory_space=pltpu.VMEM)],
+        out_specs=pl.BlockSpec(memory_space=pltpu.VMEM),
+        scratch_shapes=[
+            pltpu.VMEM((n - 1, rows, cols), x.dtype),
+            pltpu.SemaphoreType.DMA((n - 1,)),
+            pltpu.SemaphoreType.DMA((n - 1,)),
+        ],
+        compiler_params=pltpu.CompilerParams(collective_id=collective_id, has_side_effects=True),
+    )(x)
+
+
+def on_group(stride, n):
+    def place():
+        g, s = lax.axis_index("group"), lax.axis_index("shard")
+        digit = lax.rem(g // stride, n)
+        return digit, lambda at: (g + (at - digit) * stride, s)
+
+    return place
+
+
+def on_shard():
+    g, s = lax.axis_index("group"), lax.axis_index("shard")
+    return s, lambda at: (g, at)
+
+
+def on_all():
+    width = lax.axis_size("shard")
+    g, s = lax.axis_index("group"), lax.axis_index("shard")
+    return g * width + s, lambda at: (at // width, lax.rem(at, width))
+
+
+def scatter_over_group(x, first_id):
+    groups = lax.axis_size("group")
+    local, rows, cols = x.shape[0] // groups, x.shape[1], x.shape[2]
+    pairs = x.reshape(groups // 2, 2, local * rows, cols).transpose(1, 0, 2, 3)
+    pairs = pairs.reshape(2, groups // 2 * local * rows, cols)
+    half = exchange_sum(pairs, on_group(1, 2), 2, True, first_id)
+    half = half.reshape(groups // 2, local * rows, cols)
+    out = exchange_sum(half, on_group(2, groups // 2), groups // 2, True, first_id + 1)
+    return out.reshape(local, rows, cols)
+
+
 def shards(momentum, gradient, q_prev, owner_group, group_counts):
     me = lax.axis_index("group")
     experts, block, hidden = momentum.shape
@@ -33,19 +128,24 @@
     for j in range(cap):
         pick = mine & (slot_of == j)
         pieces = jnp.where(pick[:, None, None], q_prev[0, j][None], pieces)
-    q_one = lax.psum_scatter(pieces, "group", scatter_dimension=0, tiled=True)
+    q_one = scatter_over_group(pieces, 0)
     q_shard = lax.all_gather(q_one, "shard", axis=1, tiled=True)
     q_full = lax.all_gather(q_shard, "group", axis=0, tiled=True)
 
     combined = (momentum.astype(jnp.float32) + gradient.astype(jnp.float32)).astype(jnp.bfloat16)
     left_raw = jnp.einsum("erh,ehk->erk", combined, q_full, preferred_element_type=jnp.float32)
-    squares = lax.psum(jnp.sum(left_raw * left_raw, axis=1), AXES)
+    devices = lax.axis_size("group") * lax.axis_size("shard")
+    squares = exchange_sum(jnp.sum(left_raw * left_raw, axis=1), on_all, devices, False, 2)
     left_unit = (left_raw * lax.rsqrt(squares + stability_offset)[:, None, :]).astype(jnp.bfloat16)
     part = jnp.einsum("erh,erk->ehk", combined, left_unit, preferred_element_type=jnp.float32)
 
-    part = lax.psum_scatter(part, "group", scatter_dimension=0, tiled=True)
-    share = lax.psum_scatter(part, "shard", scatter_dimension=1, tiled=True)
-    right = lax.all_gather(share.astype(jnp.bfloat16), "shard", axis=1, tiled=True)
+    part = scatter_over_group(part.astype(jnp.bfloat16), 3)
+    ring = lax.axis_size("shard")
+    local = part.shape[0]
+    part = part.reshape(local, ring, share_rows, rank).transpose(1, 0, 2, 3)
+    part = part.reshape(ring, local * share_rows, rank)
+    share = exchange_sum(part, on_shard, ring, True, 5).reshape(local, share_rows, rank)
+    right = lax.all_gather(share, "shard", axis=1, tiled=True)
     right = lax.all_gather(right, "group", axis=0, tiled=True)
 
     right32 = right.astype(jnp.float32)

time: 347 us -> 258 us (0.74)
  waiting for transfers between devices: 211 us -> 72.7 us
  Pallas kernels: 0 us -> 80.2 us
  blocking collectives: 73.3 us -> 36.2 us
  local copies, waits for them, and re-layouts: 1.72 us -> 7.29 us
    reduce_scatter x3 -> x0, waiting for transfers between devices: 141 us -> none  [the longest x1 72.4 us: shards(): part = lax.psum_scatter(part, 'group', scatter_dimension=0, tiled=True)]
    pallas_call x0 -> x6, Pallas kernels: none -> 80.2 us  [exchange_sum(): pl.pallas_call(kernel, out_shape=jax.ShapeDtypeStruct((rows, cols), x.dty...]
    psum x1 -> x0, blocking collectives: 39.3 us -> none  [shards(): squares = lax.psum(jnp.sum(left_raw * left_raw, axis=1), AXES)]
    reshape x0 -> x1, local copies, waits for them, and re-layouts: none -> 4.5 us  [scatter_over_group(): pairs = x.reshape(groups // 2, 2, local * rows, cols).transpose(1, 0, 2, 3)]
  transfers between devices with their start and end apart: 5 -> 2, of which waited for: 5 -> 2; matrix products, arithmetic and copies ran while one was open for 0% -> 0% of each run, Pallas kernels for 0% -> 0%
where the time goes in v2:
time: 258 us; the launch traced here: 257 us
  Pallas kernels  80.2 us (31%)
  waiting for transfers between devices  72.7 us (28%)
  matrix products  36.3 us (14%)
  blocking collectives  36.2 us (14%)
  between operations  14.2 us (6%)
  other arithmetic  10.1 us (4%)
  local copies, waits for them, and re-layouts  7.29 us (3%)
    pallas_call x6, Pallas kernels, exchange_sum(): pl.pallas_call(kernel, out_shape=jax.ShapeDtypeStruct((rows, cols), x.dty...  80.2 us
    all_gather x1, waiting for transfers between devices, shards(): q_full = lax.all_gather(q_shard, 'group', axis=0, tiled=True)  36.5 us
    all_gather x1, waiting for transfers between devices, shards(): right = lax.all_gather(right, 'group', axis=0, tiled=True)  36.1 us
    all_gather x1, blocking collectives, shards(): right = lax.all_gather(share, 'shard', axis=1, tiled=True)  18.4 us
    all_gather x1, blocking collectives, shards(): q_shard = lax.all_gather(q_one, 'shard', axis=1, tiled=True)  17.8 us
    dot_general x1, matrix products, shards(): jnp.einsum('erk,ehk->erh', left_unit, right, preferred_element_type=jnp.f...  11.3 us
    dot_general x1, matrix products, shards(): jnp.einsum('erh,erk->ehk', combined, left_unit, preferred_element_type=jn...  10.6 us
    dot_general x1, matrix products, shards(): jnp.einsum('erh,ehk->erk', combined, q_full, preferred_element_type=jnp.f...  9.35 us
  transfers between devices with their start and end apart: 2, of which 2 were waited for; matrix products, arithmetic and copies ran while one was open for 0% of the time, Pallas kernels for 0%

profile of v2, /device:TPU:0, one launch (start us, length us, event | category | flops | bytes accessed | tf_op | source)
XLA Modules:
  0.0 257.1 jit_solution(8571426648664251801)
XLA Ops:
  7.2 0.0 copy-start
  7.2 0.0 all-gather.7.cloned.1.call-start
  7.2 0.9 convert_reduce_fusion
  8.1 0.7 compare_select_fusion
  8.8 0.0 copy-done
  8.8 0.6 gather_fusion
  9.5 0.7 compare_and_fusion.2
  10.1 0.1 broadcast_in_dim.133
  10.2 0.1 copy.18
  10.3 0.1 broadcast_bitcast_fusion
  10.4 0.1 broadcast_in_dim.124
  10.5 0.1 copy.17
  10.6 0.1 broadcast_bitcast_fusion.1
  10.7 0.1 broadcast_in_dim.115
  10.8 0.1 copy.16
  10.9 0.1 broadcast_bitcast_fusion.2
  11.0 1.1 slice_bitcast_fusion.2
  12.1 0.1 broadcast_in_dim.139
  12.2 0.1 broadcast_in_dim.130
  12.2 0.1 broadcast_in_dim.121
  12.3 4.0 %select_select_fusion.x_ref = bf16[2,2048,128]{2,1,0:T(8,128)(2,1)} fusion(pred[2,2048]{1,0:T(4,128)(4,1)S(1)} %bitcast.55, pred[2,2048]{1,0:T(4,128)(4,1)S(1)} %bitcast.56, pred[2,2048]{1,0:T(4,128)(4,1)S(1)} %bitcast.57, bf16[2048,128]{1,0:T(8,128)(2,1)S(1)} %bitcast.47, bf16[2048,128]{1,0:T(8,128)(2,1)S(1)} %bitcast.48, bf16[2048,128]{1,0:T(8,128)(2,1)S(1)} %bitcast.49), kind=kLoop, calls=%fused_computation.12 | loop fusion | flops 1572864 | bytes 2633728 | tf_op jit(solution)/shard_map/jit(_where)/select_n | solution.py:130
  16.3 4.3 %shard_map.76 = bf16[2048,128]{1,0:T(8,128)(2,1)} custom-call(bf16[2,2048,128]{2,1,0:T(8,128)(2,1)} %select_select_fusion.x_ref), custom_call_target="tpu_custom_call" | custom-call | tf_op jit(solution)/shard_map/pallas_call | solution.py:74
  20.6 12.6 %shard_map.77 = bf16[512,128]{1,0:T(8,128)(2,1)} custom-call(bf16[4,512,128]{2,1,0:T(8,128)(2,1)} %bitcast.50), custom_call_target="tpu_custom_call" | custom-call | tf_op jit(solution)/shard_map/pallas_call | solution.py:74
  33.2 17.8 %all-gather = bf16[2048,128]{1,0:T(8,128)(2,1)} all-gather(bf16[512,128]{1,0:T(8,128)(2,1)} %shard_map.77), channel_id=2, replica_groups=mesh['group'=8,'shard'=4] {'shard'}, dimensions={0}, use_global_device_ids=true | all-gather | bytes 655360 | tf_op jit(solution)/shard_map/all_gather | solution.py:132
  51.0 0.0 all-gather.7.cloned.1.call-update
  51.0 0.0 all-gather.9.cloned.1.call-start
  51.1 36.5 %all-gather.7.cloned.1.call-done = bf16[16384,128]{1,0:T(8,128)(2,1)} async-done(((bf16[2048,128]{1,0:T(8,128)(2,1)}), bf16[16384,128]{1,0:T(8,128)(2,1)}) %all-gather.7.cloned.1.call-update) | async-done | bytes 4194320 | tf_op jit(solution)/shard_map/all_gather | solution.py:133
  87.6 9.3 %multiply_reduce_fusion = (f32[8,128]{1,0:T(8,128)}, f32[8,224,128]{2,1,0:T(8,128)S(1)}) fusion(bf16[8,2048,128]{2,1,0:T(8,128)(2,1)} %bitcast.58, bf16[8,224,2048]{2,1,0:T(8,128)(2,1)} %param.6, bf16[8,224,2048]{2,1,0:T(8,128)(2,1)} %param.5), kind=kOutput, calls=%fused_computation.14 | convolution fusion | flops 954661888 | bytes 19795968 | tf_op jit(solution)/shard_map/erh,ehk->erk/dot_general | solution.py:136
  97.0 11.1 %shard_map.78 = f32[8,128]{1,0:T(8,128)} custom-call(f32[8,128]{1,0:T(8,128)} %get-tuple-element.13.x_ref), custom_call_target="tpu_custom_call" | custom-call | tf_op jit(solution)/shard_map/pallas_call | solution.py:74
  108.1 0.7 add_rsqrt_fusion.1
  108.8 0.1 multiply_convert_fusion.1
  108.9 10.6 %convolution_convert_fusion = bf16[8,2048,128]{2,1,0:T(8,128)(2,1)} fusion(bf16[8,224,128]{2,1,0:T(8,128)(2,1)S(1)} %multiply_convert_fusion.1, bf16[8,224,2048]{2,1,0:T(8,128)(2,1)} %param.6, bf16[8,224,2048]{2,1,0:T(8,128)(2,1)} %param.5), kind=kOutput, calls=%fused_computation.8 | convolution fusion | flops 956301312 | bytes 19333120 | tf_op jit(solution)/shard_map/erh,erk->ehk/dot_general | solution.py:140
  119.5 4.5 %copy.19 = bf16[4,2,2048,128]{3,2,0,1:T(8,128)(2,1)} copy(bf16[4,2,2048,128]{3,2,1,0:T(8,128)(2,1)} %bitcast.44) | data formatting | bytes 8388608 | tf_op jit(solution)/shard_map/reshape | solution.py:111
  124.0 8.5 %shard_map.79 = bf16[8192,128]{1,0:T(8,128)(2,1)} custom-call(bf16[2,8192,128]{2,1,0:T(8,128)(2,1)} %bitcast.45), custom_call_target="tpu_custom_call" | custom-call | tf_op jit(solution)/shard_map/pallas_call | solution.py:74
  132.5 28.9 %shard_map.80 = bf16[2048,128]{1,0:T(8,128)(2,1)} custom-call(bf16[4,2048,128]{2,1,0:T(8,128)(2,1)} %bitcast.46), custom_call_target="tpu_custom_call" | custom-call | tf_op jit(solution)/shard_map/pallas_call | solution.py:74
  161.4 14.8 %shard_map.81 = bf16[512,128]{1,0:T(8,128)(2,1)} custom-call(bf16[4,512,128]{2,1,0:T(8,128)(2,1)} %bitcast.51), custom_call_target="tpu_custom_call" | custom-call | tf_op jit(solution)/shard_map/pallas_call | solution.py:74
  176.2 18.4 %all-gather.2 = bf16[2048,128]{1,0:T(8,128)(2,1)} all-gather(bf16[512,128]{1,0:T(8,128)(2,1)} %shard_map.81), channel_id=4, replica_groups=mesh['group'=8,'shard'=4] {'shard'}, dimensions={0}, use_global_device_ids=true | all-gather | bytes 655360 | tf_op jit(solution)/shard_map/all_gather | solution.py:148
  194.6 0.0 all-gather.9.cloned.1.call-update
  194.6 36.1 %all-gather.9.cloned.1.call-done = bf16[16384,128]{1,0:T(8,128)(2,1)} async-done(((bf16[2048,128]{1,0:T(8,128)(2,1)}), bf16[16384,128]{1,0:T(8,128)(2,1)}) %all-gather.9.cloned.1.call-update) | async-done | bytes 4194320 | tf_op jit(solution)/shard_map/all_gather | solution.py:149
  230.8 0.0 copy-start.1
  230.8 11.3 %subtract_convert_fusion = bf16[8,224,2048]{2,1,0:T(8,128)(2,1)} fusion(bf16[8,224,128]{2,1,0:T(8,128)(2,1)S(1)} %multiply_convert_fusion.1, bf16[8,2048,128]{2,1,0:T(8,128)(2,1)} %bitcast.43, bf16[8,224,2048]{2,1,0:T(8,128)(2,1)} %param.6, bf16[8,224,2048]{2,1,0:T(8,128)(2,1)} %param.5), kind=kOutput, calls=%fused_computation.2 | convolution fusion | flops 968884224 | bytes 26673152 | tf_op jit(solution)/shard_map/erk,ehk->erh/dot_general | solution.py:158
  242.0 0.0 copy-done.1
  242.0 0.8 fusion
  242.9 0.8 fusion.1
  243.7 5.1 %multiply_convert_fusion = bf16[8,224,2048]{2,1,0:T(8,128)(2,1)} fusion(bf16[8,224,128]{2,1,0:T(8,128)(2,1)S(1)} %multiply_convert_fusion.1, bf16[8,2048,128]{2,1,0:T(8,128)(2,1)S(1)} %fusion.1), kind=kOutput, calls=%fused_computation.1 | convolution fusion | flops 946864128 | bytes 11993088 | tf_op jit(solution)/shard_map/erk,ehk->erh/dot_general | solution.py:155
  248.8 0.6 select_reduce_fusion.2
  249.4 0.8 maximum_bitcast_fusion
  (6 shorter events, 0.1 us)
Async XLA Ops:
  7.2 1.6 copy-start
  7.2 80.4 %all-gather.7.cloned.1.call-start = ((), (), s32[]{:S(2)}) async-start(), calls=%async_computation | async-start | bytes 4718592 | tf_op jit(solution)/shard_map/all_gather | solution.py:133
  51.0 179.7 %all-gather.9.cloned.1.call-start = ((), (), s32[]{:S(2)}) async-start(), calls=%async_computation.1 | async-start | bytes 4718592 | tf_op jit(solution)/shard_map/all_gather | solution.py:149
  230.8 11.3 %copy-start.1 = (bf16[16384,128]{1,0:T(8,128)(2,1)S(1)}, bf16[16384,128]{1,0:T(8,128)(2,1)}, u32[]{:S(2)}) copy-start(bf16[16384,128]{1,0:T(8,128)(2,1)} %all-gather.9.cloned.1.call-done) | copy-start | bytes 12582916
Sparse Core Ops, SparseCore 0:
  51.2 36.4 all-gather.6
  194.7 35.9 all-gather.8
